TPU v7x, 256 devices: a whole 4x4x8 slice. The times are simulated.
256 devices in a mesh: tok: 8 (over x, core), voc: 32 (over z, y).
Axes of the slice: x: 4, y: 4, z: 8, core: 2. Of those that a mesh axis runs over, the one named last changes fastest.
Arguments:
- hidden_rows: bfloat16 [1024, 8192], P('tok', 'voc'), may hold values from -2 to 2
- teacher_weight: bfloat16 [8192, 152064], P(None, ('tok', 'voc')), may hold values from -64 to 64
- student_logits: bfloat16 [1024, 128256], P('tok', 'voc'), may hold values from -8 to 300
- slot_source: int32 [32, 32, 256], P('voc'), may hold values from -1 to 4751, as said below
- slot_target: int32 [32, 32, 256], P('voc'), may hold values from -1 to 4007, as said below
Outputs:
- loss: float32 [1024], P('tok')
- student_grad: bfloat16 [1024, 128256], P('tok', 'voc')
Inputs may be any that keep to these rules, and one draw needn't show every extreme that they name: Each of the 4752 local columns of group g appears in exactly one slot of slot_source[g]; all other slots hold -1. One owner's 256 slots are filled in every group. slot_target[j, g, c] is -1 exactly where slot_source[g, j, c] is -1.
All inputs are finite; a program needn't handle non-finite values.
Results may differ from a plain program's by a relative error of at most 0.0022.
The roundings to bfloat16 on the way count: a program that leaves them out, or rounds other values in their place, can miss the bound.
Values may be sent and summed in bfloat16 or wider, within the bound.
No kernel may reach another device: no remote copies, remote signals or barrier semaphores. Data moves between devices by JAX's collectives and lax.ppermute only.
A program may use at most 128 MiB of HBM per device.

v0:
```python
import jax
import jax.numpy as jnp
from jax import lax
from jax.sharding import Mesh
from jax.sharding import PartitionSpec as P

VOC = ("voc_0", "voc_1")
TOK = ("tok_0", "tok_1")
TOK_VOC = ("tok_0", "tok_1", "voc_0", "voc_1")


def gathered_by_axis(value, axes, dim):
    if not axes:
        return value
    nearer = lax.all_gather(value, axes[-1], axis=dim, tiled=True)
    return gathered_by_axis(nearer, axes[:-1], dim)


def collected_together(value, axis):
    leaves = jax.tree.leaves(value)
    order = sorted(range(len(leaves)), key=lambda k: -leaves[k].size)
    width = (1, *leaves[order[0]].shape)[-1]
    lines = [
        jnp.pad(leaves[k].reshape(-1), (0, -leaves[k].size % width)).reshape(-1, width)
        for k in order
    ]
    both, at, found = (lax.all_gather(jnp.concatenate(lines), axis), 0, {})
    for k, line in zip(order, lines):
        slab = both[:, at : at + len(line)].reshape(len(both), -1)
        found[k] = slab[:, : leaves[k].size].reshape(-1, *leaves[k].shape)
        at += len(line)
    numbers = iter(range(len(leaves)))
    return jax.tree.map(lambda _: found[next(numbers)], value)


def joined_all(value, axes, combine):
    for axis in axes:
        pieces = collected_together(value, axis)
        value = jax.tree.map(lambda part: part[0], pieces)
        for k in range(1, lax.axis_size(axis)):
            value = combine(value, jax.tree.map(lambda part: part[k], pieces))
    return value


def copy_for_each(value, axis):
    copies = jnp.broadcast_to(value, (lax.axis_size(axis), *value.shape))
    return lax.all_to_all(copies, axis, split_axis=0, concat_axis=0, tiled=True)


def gathered_once(value, axis):
    leaves = jax.tree.leaves(value)
    order = sorted(range(len(leaves)), key=lambda k: -leaves[k].size)
    width = (1, *leaves[order[0]].shape)[-1]
    lines = [
        jnp.pad(leaves[k].reshape(-1), (0, -leaves[k].size % width)).reshape(-1, width)
        for k in order
    ]
    both, at, found = (copy_for_each(jnp.concatenate(lines), axis), 0, {})
    for k, line in zip(order, lines):
        slab = both[:, at : at + len(line)].reshape(len(both), -1)
        found[k] = slab[:, : leaves[k].size].reshape(-1, *leaves[k].shape)
        at += len(line)
    numbers = iter(range(len(leaves)))
    return jax.tree.map(lambda _: found[next(numbers)], value)


def combined_pairwise(pieces, combine):
    while len(jax.tree.leaves(pieces)[0]) > 1:
        pieces = jax.vmap(combine)(
            *(jax.tree.map(lambda part: part[side::2], pieces) for side in (0, 1))
        )
    return jax.tree.map(lambda part: part[0], pieces)


def combined_all(value, axis, combine):
    pieces = gathered_once(value, axis)
    return combined_pairwise(pieces, combine)


def teacher_combine(first, second):
    highest = jnp.maximum(first[0], second[0])
    summed = first[1] * jnp.exp(first[0] - highest) + second[1] * jnp.exp(second[0] - highest)
    return (highest, summed)


def student_combine(first, second):
    highest = jnp.maximum(first[0], second[0])
    summed = first[1] * jnp.exp(first[0] - highest) + second[1] * jnp.exp(second[0] - highest)
    return (highest, summed, first[2] + second[2], first[3] + second[3])


def shards(hidden_rows, teacher_weight, student_logits, slot_source, slot_target):
    full_rows = gathered_by_axis(hidden_rows, VOC, 1)
    logits = jnp.dot(
        lax.all_gather(full_rows, TOK, axis=0, tiled=True),
        teacher_weight,
        preferred_element_type=jnp.float32,
    )
    local_max = jnp.max(logits, axis=1)
    shifted_local = jnp.exp(logits - local_max[:, None])
    teacher_max, teacher_total = joined_all(
        (local_max, jnp.sum(shifted_local, axis=1)), TOK_VOC, teacher_combine
    )
    shifted = shifted_local * jnp.exp(local_max - teacher_max)[:, None]
    probs = (shifted / teacher_total[:, None]).astype(jnp.bfloat16)
    grouped = lax.all_to_all(probs, TOK, split_axis=0, concat_axis=1, tiled=True)
    source = slot_source[0]
    flat_source = source.reshape(-1)
    picked = jnp.take(grouped, jnp.maximum(flat_source, 0), axis=1)
    picked = jnp.where((flat_source >= 0)[None, :], picked, jnp.zeros_like(picked))
    outgoing = picked.reshape(grouped.shape[0], source.shape[0], source.shape[1])
    width = student_logits.shape[1]
    target = slot_target[0].reshape(-1)
    column = jnp.where(target >= 0, target, width)
    arrived = lax.all_to_all(outgoing, VOC, split_axis=1, concat_axis=1, tiled=True)
    values = arrived.reshape(arrived.shape[0], -1).astype(jnp.float32)
    folded = (
        jnp.zeros((arrived.shape[0], width), jnp.float32).at[:, column].add(values, mode="drop")
    )
    student = student_logits.astype(jnp.float32)
    own_max = jnp.max(student, axis=1)
    own_total = jnp.sum(jnp.exp(student - own_max[:, None]), axis=1)
    cross = jnp.sum(folded * student, axis=1)
    weight_mass = jnp.sum(folded, axis=1)
    student_max, student_total, cross, weight_mass = combined_all(
        (own_max, own_total, cross, weight_mass), VOC, student_combine
    )
    student_lse = student_max + jnp.log(student_total)
    loss = student_lse * weight_mass - cross
    student_grad = (jnp.exp(student - student_lse[:, None]) - folded).astype(jnp.bfloat16)
    return (loss, student_grad)


def solution(mesh):
    finer = Mesh(mesh.devices.reshape(4, 2, 8, 4), ("tok_0", "tok_1", "voc_0", "voc_1"))
    placed = (P(TOK, VOC), P(None, TOK_VOC), P(TOK, VOC), P(VOC, None, None), P(VOC, None, None))
    return jax.shard_map(
        shards, mesh=finer, in_specs=placed, out_specs=(P(TOK), P(TOK, VOC)), check_vma=False
    )
```

profile of v0, /device:TPU:2, one launch (start us, length us, event | category | flops | bytes accessed | tf_op | source)
XLA Modules:
  0.0 400.6 jit_solution(5841360051451919552)
XLA Ops:
  7.2 0.0 all-gather.11.cloned.1.call-start
  7.2 14.5 %all_gather.33 = bf16[128,1024]{1,0:T(8,128)(2,1)} all-gather(bf16[128,256]{1,0:T(8,128)(2,1)} %param.5), channel_id=1, replica_groups=mesh['tok_0'=4,'tok_1'=2,'voc_0'=8,'voc_1'=4] {'voc_1'}, dimensions={1}, use_global_device_ids=true | all-gather | bytes 327680 | tf_op jit(solution)/shard_map/all_gather | solution.py:15
  21.7 0.0 all-gather.11.cloned.1.call-update
  21.7 0.0 all-gather.13.cloned.1.call-start
  21.7 42.5 %all-gather.11.cloned.1.call-done = bf16[128,8192]{1,0:T(8,128)(2,1)} async-done(((bf16[128,1024]{1,0:T(8,128)(2,1)}), bf16[128,8192]{1,0:T(8,128)(2,1)}) %all-gather.11.cloned.1.call-update) | async-done | bytes 2097168 | tf_op jit(solution)/shard_map/all_gather | solution.py:15
  64.3 87.5 %all-gather.13.cloned.1.call-done = bf16[1024,8192]{1,0:T(8,128)(2,1)} async-done(((bf16[128,8192]{1,0:T(8,128)(2,1)}), bf16[1024,8192]{1,0:T(8,128)(2,1)}) %all-gather.13.cloned.1.call-update) | async-done | bytes 16777232 | tf_op jit(solution)/shard_map/all_gather | solution.py:95
  151.7 15.5 %fusion.61 = (f32[1024]{0:T(1024)S(1)}, f32[1024,594]{0,1:T(8,128)S(1)}) fusion(bf16[1024,8192]{1,0:T(8,128)(2,1)} %all-gather.13.cloned.1.call-done, bf16[8192,594]{0,1:T(8,128)(2,1)} %param.6), kind=kOutput, calls=%fused_computation.118 | convolution fusion | flops 9966273536 | bytes 28946432 | tf_op jit(solution)/shard_map/dot_general | solution.py:94
  167.3 0.4 fusion.1
  167.7 10.8 %all-gather.4 = f32[4,2,1024]{2,1,0:T(2,128)S(1)} all-gather(f32[1,2,1024]{2,1,0:T(2,128)S(1)} %maximum_bitcast_fusion.1), channel_id=2, replica_groups=mesh['tok_0'=4,'tok_1'=2,'voc_0'=8,'voc_1'=4] {'tok_0'}, dimensions={0}, use_global_device_ids=true | all-gather | bytes 40960 | tf_op jit(solution)/shard_map/all_gather | solution.py:27
  178.5 0.1 fusion.34
  178.5 1.8 all-gather.5
  180.4 26.3 %all-gather.6 = f32[8,2,1024]{2,1,0:T(2,128)S(1)} all-gather(f32[1,2,1024]{2,1,0:T(2,128)S(1)} %maximum_bitcast_fusion.3), channel_id=4, replica_groups=mesh['tok_0'=4,'tok_1'=2,'voc_0'=8,'voc_1'=4] {'voc_0'}, dimensions={0}, use_global_device_ids=true | all-gather | bytes 73728 | tf_op jit(solution)/shard_map/all_gather | solution.py:27
  206.7 0.1 fusion.10
  206.8 12.3 %all-gather.7 = f32[4,2,1024]{2,1,0:T(2,128)S(1)} all-gather(f32[1,2,1024]{2,1,0:T(2,128)S(1)} %maximum_bitcast_fusion.4), channel_id=5, replica_groups=mesh['tok_0'=4,'tok_1'=2,'voc_0'=8,'voc_1'=4] {'voc_1'}, dimensions={0}, use_global_device_ids=true | all-gather | bytes 40960 | tf_op jit(solution)/shard_map/all_gather | solution.py:27
  219.1 0.5 divide_convert_fusion
  219.6 0.3 copy.13
  219.9 0.1 slice_bitcast_fusion
  220.0 1.2 copy.9
  221.2 5.3 %all-to-all-start = ((bf16[8,128,594]{1,2,0:T(8,128)(2,1)}), bf16[8,128,594]{1,2,0:T(8,128)(2,1)S(1)}, u32[]{:S(2)}, u32[]{:S(2)}) async-start(bf16[8,128,594]{1,2,0:T(8,128)(2,1)} %copy.9), calls=%async_computation | async-start | bytes 2457600 | tf_op jit(solution)/shard_map/all_to_all | solution.py:106
  226.6 16.4 %all-to-all-done = bf16[8,128,594]{1,2,0:T(8,128)(2,1)S(1)} async-done(((bf16[8,128,594]{1,2,0:T(8,128)(2,1)}), bf16[8,128,594]{1,2,0:T(8,128)(2,1)S(1)}, u32[]{:S(2)}, u32[]{:S(2)}) %all-to-all-start) | async-done | bytes 1216544 | tf_op jit(solution)/shard_map/all_to_all | solution.py:106
  242.9 0.4 all_to_all.23
  243.3 24.0 %gather_fusion = bf16[8192,128]{1,0:T(8,128)(2,1)S(1)} fusion(bf16[128,4752]{0,1:T(8,128)(2,1)S(1)} %all_to_all.23, s32[8192]{0:T(1024)S(1)} %broadcast_clamp_fusion), kind=kCustom, calls=%fused_computation | custom fusion | bytes 4227072 | tf_op jit(solution)/shard_map/jit(_take)/gather | solution.py:109
  267.3 4.6 %select_select_fusion = bf16[128,32,256]{0,2,1:T(8,128)(2,1)} fusion(bf16[128,32,256]{0,2,1:T(8,128)(2,1)S(1)} %bitcast.322, pred[32,256]{1,0:T(8,128)(4,1)S(1)} %get-tuple-element.26, pred[32,256]{1,0:T(8,128)(4,1)S(1)} %get-tuple-element.25), kind=kLoop, calls=%fused_computation.10 | loop fusion | flops 2097152 | bytes 4210688 | tf_op jit(solution)/shard_map/jit(_where)/select_n | solution.py:110
  271.9 8.0 %all-to-all-start.1 = ((bf16[128,32,256]{0,2,1:T(8,128)(2,1)}), bf16[128,32,256]{0,2,1:T(8,128)(2,1)}, u32[]{:S(2)}, u32[]{:S(2)}) async-start(bf16[128,32,256]{0,2,1:T(8,128)(2,1)} %select_select_fusion), calls=%async_computation.1 | async-start | bytes 4194304 | tf_op jit(solution)/shard_map/all_to_all | solution.py:115
  280.0 0.5 reduce_max.27
  280.6 0.1 compare_select_fusion
  280.6 49.2 %all-to-all-done.1 = bf16[128,32,256]{0,2,1:T(8,128)(2,1)} async-done(((bf16[128,32,256]{0,2,1:T(8,128)(2,1)}), bf16[128,32,256]{0,2,1:T(8,128)(2,1)}, u32[]{:S(2)}, u32[]{:S(2)}) %all-to-all-start.1) | async-done | bytes 2097184 | tf_op jit(solution)/shard_map/all_to_all | solution.py:115
  329.8 45.0 %scatter_custom_fusion = f32[128,4008]{0,1:T(8,128)S(1)} fusion(s32[8192]{0:T(1024)S(1)} %bitcast.338, bf16[128,8192]{0,1:T(8,128)(2,1)} %bitcast.62, f32[]{:T(128)} %constant.10.clone.1), kind=kCustom, calls=%fused_computation.3 | custom fusion | flops 2097152 | bytes 4149252 | tf_op jit(solution)/shard_map/scatter-add | solution.py:118
  374.9 0.6 fusion.4
  375.4 15.7 %all_to_all.29 = f32[32,4,128]{2,1,0:T(4,128)S(1)} all-to-all(f32[32,4,128]{2,1,0:T(4,128)S(1)} %broadcast_in_dim.44), channel_id=1, replica_groups=mesh['tok_0'=4,'tok_1'=2,'voc_0'=8,'voc_1'=4] {'voc_0','voc_1'}, dimensions={0} | all-to-all | bytes 131072 | tf_op jit(solution)/shard_map/all_to_all | solution.py:47
  391.9 0.5 bitcast_subtract_fusion
  392.4 1.4 fusion.7
  (67 shorter events, 0.9 us)
Async XLA Ops:
  7.2 57.1 %all-gather.11.cloned.1.call-start = ((), (), s32[]{:S(2)}) async-start(), calls=%async_computation.3 | async-start | bytes 2359296 | tf_op jit(solution)/shard_map/all_gather | solution.py:15
  21.7 130.0 %all-gather.13.cloned.1.call-start = ((), (), s32[]{:S(2)}) async-start(), calls=%async_computation.4 | async-start | bytes 18874368 | tf_op jit(solution)/shard_map/all_gather | solution.py:95
  220.0 6.5 %copy-start.1 = (s32[1,32,256]{2,1,0:T(8,128)S(1)}, s32[1,32,256]{2,1,0:T(8,128)}, u32[]{:S(2)}) copy-start(s32[1,32,256]{2,1,0:T(8,128)} %param.8) | copy-start | bytes 98308
  221.2 21.7 %all-to-all-start = ((bf16[8,128,594]{1,2,0:T(8,128)(2,1)}), bf16[8,128,594]{1,2,0:T(8,128)(2,1)S(1)}, u32[]{:S(2)}, u32[]{:S(2)}) async-start(bf16[8,128,594]{1,2,0:T(8,128)(2,1)} %copy.9), calls=%async_computation | async-start | bytes 2457600 | tf_op jit(solution)/shard_map/all_to_all | solution.py:106
  271.9 8.1 %copy-start.2 = (s32[1,32,256]{2,1,0:T(8,128)S(1)}, s32[1,32,256]{2,1,0:T(8,128)}, u32[]{:S(2)}) copy-start(s32[1,32,256]{2,1,0:T(8,128)} %param.9) | copy-start | bytes 98308
  271.9 8.1 %copy-start = (bf16[128,4008]{0,1:T(8,128)(2,1)S(1)}, bf16[128,4008]{0,1:T(8,128)(2,1)}, u32[]{:S(2)}) copy-start(bf16[128,4008]{0,1:T(8,128)(2,1)} %param.7) | copy-start | bytes 3078148
  271.9 57.9 %all-to-all-start.1 = ((bf16[128,32,256]{0,2,1:T(8,128)(2,1)}), bf16[128,32,256]{0,2,1:T(8,128)(2,1)}, u32[]{:S(2)}, u32[]{:S(2)}) async-start(bf16[128,32,256]{0,2,1:T(8,128)(2,1)} %select_select_fusion), calls=%async_computation.1 | async-start | bytes 4194304 | tf_op jit(solution)/shard_map/all_to_all | solution.py:115
Sparse Core Ops, SparseCore 0:
  21.8 42.3 all-gather.10
  66.1 85.6 all-gather.12
where the time goes:
time: 401 us
  waiting for transfers between devices  196 us (49%)
  blocking collectives  81.3 us (20%)
  other arithmetic  53.9 us (13%)
  local copies, waits for them, and re-layouts  26.6 us (7%)
  matrix products  15.5 us (4%)
  between operations  14.3 us (4%)
  starting transfers between devices  13.4 us (3%)
    all_gather x1, waiting for transfers between devices, shards(): lax.all_gather(full_rows, TOK, axis=0, tiled=True)  87.5 us
    all_gather x4, blocking collectives, collected_together(): both, at, found = (lax.all_gather(jnp.concatenate(lines), axis), 0, {})  51.1 us
    all_to_all x1, waiting for transfers between devices, shards(): lax.all_to_all(outgoing, VOC, split_axis=1, concat_axis=1, tiled=True)  49.2 us
    scatter-add x1, other arithmetic, shards(): jnp.zeros((arrived.shape[0], width), jnp.float32).at[:, column]  45 us
    all_gather x1, waiting for transfers between devices, gathered_by_axis(): nearer = lax.all_gather(value, axes[-1], axis=dim, tiled=True)  42.5 us
    gather x1, local copies, waits for them, and re-layouts, shards(): picked = jnp.take(grouped, jnp.maximum(flat_source, 0), axis=1)  24 us
    all_to_all x1, waiting for transfers between devices, shards(): lax.all_to_all(probs, TOK, split_axis=0, concat_axis=1, tiled=True)  16.4 us
    all_to_all x1, blocking collectives, copy_for_each(): return lax.all_to_all(copies, axis, split_axis=0, concat_axis=0, tiled=True)  15.7 us
  transfers between devices with their start and end apart: 4, of which 4 were waited for; matrix products, arithmetic and copies ran while one was open for 0% of the time, Pallas kernels for 0%

commit v1 on v0

--- a/solution.py
+++ b/solution.py
@@ -91,10 +91,17 @@
 
 def shards(hidden_rows, teacher_weight, student_logits, slot_source, slot_target):
     full_rows = gathered_by_axis(hidden_rows, VOC, 1)
+    lead_joints_for = lambda z, row_dim: jnp.concatenate(
+        jax.lax.all_to_all(
+            jnp.stack([z for _ in range(jax.lax.axis_size(TOK))], 0),
+            axis_name=TOK,
+            split_axis=0,
+            concat_axis=0,
+        ),
+        row_dim,
+    )
     logits = jnp.dot(
-        lax.all_gather(full_rows, TOK, axis=0, tiled=True),
-        teacher_weight,
-        preferred_element_type=jnp.float32,
+        lead_joints_for(full_rows, row_dim=0), teacher_weight, preferred_element_type=jnp.float32
     )
     local_max = jnp.max(logits, axis=1)
     shifted_local = jnp.exp(logits - local_max[:, None])

time: 401 us -> 507 us (1.26)
  blocking collectives: 81.3 us -> 270 us
  waiting for transfers between devices: 196 us -> 108 us
    all_to_all x0 -> x1, blocking collectives: none -> 190 us  [shards(): jax.lax.all_to_all(jnp.stack([z for _ in range(jax.lax.axis_size(TOK))],...]
    all_gather x1 -> x0, waiting for transfers between devices: 87.5 us -> none  [shards(): lax.all_gather(full_rows, TOK, axis=0, tiled=True)]
  transfers between devices with their start and end apart: 4 -> 3, of which waited for: 4 -> 3; matrix products, arithmetic and copies ran while one was open for 0% -> 0% of each run, Pallas kernels for 0% -> 0%
where the time goes in v1:
time: 507 us; the launch traced here: 506 us
  blocking collectives  270 us (53%)
  waiting for transfers between devices  108 us (21%)
  other arithmetic  53.9 us (11%)
  local copies, waits for them, and re-layouts  30.4 us (6%)
  matrix products  18.8 us (4%)
  between operations  14.3 us (3%)
  starting transfers between devices  11.3 us (2%)
    all_to_all x1, blocking collectives, shards(): jax.lax.all_to_all(jnp.stack([z for _ in range(jax.lax.axis_size(TOK))],...  190 us
    all_gather x4, blocking collectives, collected_together(): both, at, found = (lax.all_gather(jnp.concatenate(lines), axis), 0, {})  49.4 us
    all_to_all x1, waiting for transfers between devices, shards(): lax.all_to_all(outgoing, VOC, split_axis=1, concat_axis=1, tiled=True)  49.2 us
    scatter-add x1, other arithmetic, shards(): jnp.zeros((arrived.shape[0], width), jnp.float32).at[:, column]  45 us
    all_gather x1, waiting for transfers between devices, gathered_by_axis(): nearer = lax.all_gather(value, axes[-1], axis=dim, tiled=True)  42.5 us
    gather x1, local copies, waits for them, and re-layouts, shards(): picked = jnp.take(grouped, jnp.maximum(flat_source, 0), axis=1)  24 us
    dot_general x1, matrix products, shards(): jnp.dot(lead_joints_for(full_rows, row_dim=0), teacher_weight, preferred_...  18.8 us
    all_to_all x1, waiting for transfers between devices, shards(): lax.all_to_all(probs, TOK, split_axis=0, concat_axis=1, tiled=True)  16.3 us
  transfers between devices with their start and end apart: 3, of which 3 were waited for; matrix products, arithmetic and copies ran while one was open for 0% of the time, Pallas kernels for 0%

profile of v1, /device:TPU:2, one launch (start us, length us, event | category | flops | bytes accessed | tf_op | source)
XLA Modules:
  0.0 506.4 jit_solution(9828562998895494294)
XLA Ops:
  7.2 0.0 all-gather.10.cloned.1.call-start
  7.2 14.5 %all_gather.30 = bf16[128,1024]{1,0:T(8,128)(2,1)} all-gather(bf16[128,256]{1,0:T(8,128)(2,1)} %param.5), channel_id=1, replica_groups=mesh['tok_0'=4,'tok_1'=2,'voc_0'=8,'voc_1'=4] {'voc_1'}, dimensions={1}, use_global_device_ids=true | all-gather | bytes 327680 | tf_op jit(solution)/shard_map/all_gather | solution.py:15
  21.7 0.0 all-gather.10.cloned.1.call-update
  21.7 42.5 %all-gather.10.cloned.1.call-done = bf16[128,8192]{1,0:T(8,128)(2,1)} async-done(((bf16[128,1024]{1,0:T(8,128)(2,1)}), bf16[128,8192]{1,0:T(8,128)(2,1)}) %all-gather.10.cloned.1.call-update) | async-done | bytes 2097168 | tf_op jit(solution)/shard_map/all_gather | solution.py:15
  64.2 3.8 stack.2
  68.0 190.0 %all_to_all.34 = bf16[8,128,8192]{2,1,0:T(8,128)(2,1)S(1)} all-to-all(bf16[8,128,8192]{2,1,0:T(8,128)(2,1)S(1)} %stack.2), channel_id=1, replica_groups=mesh['tok_0'=4,'tok_1'=2,'voc_0'=8,'voc_1'=4] {'tok_0','tok_1'}, dimensions={0} | all-to-all | bytes 33554432 | tf_op jit(solution)/shard_map/all_to_all | solution.py:95
  258.0 18.8 %fusion.61 = (f32[1024]{0:T(1024)S(1)}, f32[1024,594]{0,1:T(8,128)S(1)}) fusion(bf16[1024,8192]{1,0:T(8,128)(2,1)S(1)} %bitcast.323, bf16[8192,594]{0,1:T(8,128)(2,1)} %param.6), kind=kOutput, calls=%fused_computation.118 | convolution fusion | flops 9966273536 | bytes 28946432 | tf_op jit(solution)/shard_map/dot_general | solution.py:103
  276.8 0.4 fusion.1
  277.2 10.7 %all-gather.4 = f32[4,2,1024]{2,1,0:T(2,128)S(1)} all-gather(f32[1,2,1024]{2,1,0:T(2,128)S(1)} %maximum_bitcast_fusion.1), channel_id=2, replica_groups=mesh['tok_0'=4,'tok_1'=2,'voc_0'=8,'voc_1'=4] {'tok_0'}, dimensions={0}, use_global_device_ids=true | all-gather | bytes 40960 | tf_op jit(solution)/shard_map/all_gather | solution.py:27
  287.9 0.1 fusion.34
  288.0 1.8 all-gather.5
  289.8 24.6 %all-gather.6 = f32[8,2,1024]{2,1,0:T(2,128)S(1)} all-gather(f32[1,2,1024]{2,1,0:T(2,128)S(1)} %maximum_bitcast_fusion.3), channel_id=4, replica_groups=mesh['tok_0'=4,'tok_1'=2,'voc_0'=8,'voc_1'=4] {'voc_0'}, dimensions={0}, use_global_device_ids=true | all-gather | bytes 73728 | tf_op jit(solution)/shard_map/all_gather | solution.py:27
  314.4 0.1 fusion.10
  314.5 12.3 %all-gather.7 = f32[4,2,1024]{2,1,0:T(2,128)S(1)} all-gather(f32[1,2,1024]{2,1,0:T(2,128)S(1)} %maximum_bitcast_fusion.4), channel_id=5, replica_groups=mesh['tok_0'=4,'tok_1'=2,'voc_0'=8,'voc_1'=4] {'voc_1'}, dimensions={0}, use_global_device_ids=true | all-gather | bytes 40960 | tf_op jit(solution)/shard_map/all_gather | solution.py:27
  326.9 0.5 divide_convert_fusion
  327.3 0.3 copy.13
  327.7 0.1 slice_bitcast_fusion
  327.8 1.2 copy.9
  329.0 4.5 all-to-all-start.1
  333.6 16.3 %all-to-all-done.1 = bf16[8,128,594]{1,2,0:T(8,128)(2,1)S(1)} async-done(((bf16[8,128,594]{1,2,0:T(8,128)(2,1)}), bf16[8,128,594]{1,2,0:T(8,128)(2,1)S(1)}, u32[]{:S(2)}, u32[]{:S(2)}) %all-to-all-start.1) | async-done | bytes 1216544 | tf_op jit(solution)/shard_map/all_to_all | solution.py:113
  349.9 0.4 all_to_all.27
  350.3 24.0 %gather_fusion = bf16[8192,128]{1,0:T(8,128)(2,1)S(1)} fusion(bf16[128,4752]{0,1:T(8,128)(2,1)S(1)} %all_to_all.27, s32[8192]{0:T(1024)S(1)} %broadcast_clamp_fusion), kind=kCustom, calls=%fused_computation | custom fusion | bytes 4227072 | tf_op jit(solution)/shard_map/jit(_take)/gather | solution.py:116
  374.3 4.6 select_select_fusion
  378.9 6.8 %all-to-all-start.2 = ((bf16[128,32,256]{0,2,1:T(8,128)(2,1)}), bf16[128,32,256]{0,2,1:T(8,128)(2,1)}, u32[]{:S(2)}, u32[]{:S(2)}) async-start(bf16[128,32,256]{0,2,1:T(8,128)(2,1)} %select_select_fusion), calls=%async_computation.2 | async-start | bytes 4194304 | tf_op jit(solution)/shard_map/all_to_all | solution.py:122
  385.8 0.5 reduce_max.27
  386.3 0.1 compare_select_fusion
  386.4 49.2 %all-to-all-done.2 = bf16[128,32,256]{0,2,1:T(8,128)(2,1)} async-done(((bf16[128,32,256]{0,2,1:T(8,128)(2,1)}), bf16[128,32,256]{0,2,1:T(8,128)(2,1)}, u32[]{:S(2)}, u32[]{:S(2)}) %all-to-all-start.2) | async-done | bytes 2097184 | tf_op jit(solution)/shard_map/all_to_all | solution.py:122
  435.5 45.0 %scatter_custom_fusion = f32[128,4008]{0,1:T(8,128)S(1)} fusion(s32[8192]{0:T(1024)S(1)} %bitcast.340, bf16[128,8192]{0,1:T(8,128)(2,1)} %bitcast.63, f32[]{:T(128)} %constant.10.clone.1), kind=kCustom, calls=%fused_computation.3 | custom fusion | flops 2097152 | bytes 4149252 | tf_op jit(solution)/shard_map/scatter-add | solution.py:125
  480.6 0.6 fusion.4
  481.2 15.7 %all_to_all.35 = f32[32,4,128]{2,1,0:T(4,128)S(1)} all-to-all(f32[32,4,128]{2,1,0:T(4,128)S(1)} %broadcast_in_dim.44), channel_id=1, replica_groups=mesh['tok_0'=4,'tok_1'=2,'voc_0'=8,'voc_1'=4] {'voc_0','voc_1'}, dimensions={0} | all-to-all | bytes 131072 | tf_op jit(solution)/shard_map/all_to_all | solution.py:47
  497.6 0.5 bitcast_subtract_fusion
  498.1 1.4 fusion.7
  (66 shorter events, 0.9 us)
Async XLA Ops:
  7.2 57.1 %all-gather.10.cloned.1.call-start = ((), (), s32[]{:S(2)}) async-start(), calls=%async_computation.4 | async-start | bytes 2359296 | tf_op jit(solution)/shard_map/all_gather | solution.py:15
  327.8 5.7 %copy-start.1 = (s32[1,32,256]{2,1,0:T(8,128)S(1)}, s32[1,32,256]{2,1,0:T(8,128)}, u32[]{:S(2)}) copy-start(s32[1,32,256]{2,1,0:T(8,128)} %param.8) | copy-start | bytes 98308
  329.0 20.9 %all-to-all-start.1 = ((bf16[8,128,594]{1,2,0:T(8,128)(2,1)}), bf16[8,128,594]{1,2,0:T(8,128)(2,1)S(1)}, u32[]{:S(2)}, u32[]{:S(2)}) async-start(bf16[8,128,594]{1,2,0:T(8,128)(2,1)} %copy.9), calls=%async_computation.1 | async-start | bytes 2457600 | tf_op jit(solution)/shard_map/all_to_all | solution.py:113
  378.9 6.8 %copy-start.2 = (s32[1,32,256]{2,1,0:T(8,128)S(1)}, s32[1,32,256]{2,1,0:T(8,128)}, u32[]{:S(2)}) copy-start(s32[1,32,256]{2,1,0:T(8,128)} %param.9) | copy-start | bytes 98308
  378.9 6.8 %copy-start = (bf16[128,4008]{0,1:T(8,128)(2,1)S(1)}, bf16[128,4008]{0,1:T(8,128)(2,1)}, u32[]{:S(2)}) copy-start(bf16[128,4008]{0,1:T(8,128)(2,1)} %param.7) | copy-start | bytes 3078148
  378.9 56.6 %all-to-all-start.2 = ((bf16[128,32,256]{0,2,1:T(8,128)(2,1)}), bf16[128,32,256]{0,2,1:T(8,128)(2,1)}, u32[]{:S(2)}, u32[]{:S(2)}) async-start(bf16[128,32,256]{0,2,1:T(8,128)(2,1)} %select_select_fusion), calls=%async_computation.2 | async-start | bytes 4194304 | tf_op jit(solution)/shard_map/all_to_all | solution.py:122
Sparse Core Ops, SparseCore 0:
  21.8 42.3 all-gather.9
